TPU v7x, 16 devices: a 4x2x1 block of a 4x4x8 slice. The times are simulated.
16 devices in a mesh: dp: 2 (over y, z), tp: 8 (over x, core).
Axes of the slice: x: 4, y: 2, z: 1, core: 2. Of those that a mesh axis runs over, the one named last changes fastest.
The devices are a block of a 4x4x8 slice.
Arguments:
- x: bfloat16 [4096, 4096], P(('dp', 'tp')), parts along dimension 0
- w_gate: bfloat16 [4096, 16384], P(None, 'tp')
- w_up: bfloat16 [4096, 16384], P(None, 'tp')
- w_down: bfloat16 [16384, 4096], P('tp')
Outputs:
- output: bfloat16 [4096, 4096], P(('dp', 'tp')), parts along dimension 0
There are 2 independent parts. A program takes and returns all parts, laid end to end along the dimension named above; an argument that names none is the same for every part.
All inputs are finite; a program needn't handle non-finite values.
Results may differ from a plain program's by a relative error of at most 0.016.
Values are sent between devices in bfloat16 or wider.
A program may use at most 768 MiB of HBM per device.

v0:
```python
import jax
import jax.numpy as jnp
from jax import lax
from jax.sharding import PartitionSpec as P


def solution(mesh):
    def step(x, w_gate, w_up, w_down):
        rows = lax.all_gather(x, "tp", axis=0, tiled=True)
        gate = jnp.dot(rows, w_gate, preferred_element_type=jnp.float32)
        up = jnp.dot(rows, w_up, preferred_element_type=jnp.float32)
        hidden = (jax.nn.silu(gate) * up).astype(jnp.bfloat16)
        term = jnp.dot(hidden, w_down, preferred_element_type=jnp.float32).astype(jnp.bfloat16)
        return lax.psum_scatter(term, "tp", scatter_dimension=0, tiled=True)

    return jax.shard_map(
        step,
        mesh=mesh,
        in_specs=(P(("dp", "tp"), None), P(None, "tp"), P(None, "tp"), P("tp", None)),
        out_specs=P(("dp", "tp"), None),
        check_vma=False,
    )
```

profile of v0, /device:TPU:112, one launch (start us, length us, event | category | flops | bytes accessed | tf_op | source)
XLA Modules:
  0.0 319.0 jit_solution(17479161485801976132)
XLA Ops:
  6.5 0.0 all-gather.2.cloned.1.call-start
  6.6 0.7 all-gather.2.cloned.1.call-update
  7.3 0.1 reduce-scatter.2.cloned.1.call-start
  7.4 85.5 %all-gather.2.cloned.1.call-done = bf16[2048,4096]{1,0:T(8,128)(2,1)} async-done(((bf16[256,4096]{1,0:T(8,128)(2,1)}), bf16[2048,4096]{1,0:T(8,128)(2,1)}) %all-gather.2.cloned.1.call-update) | async-done | bytes 16777232 | tf_op jit(solution)/shard_map/all_gather | solution.py:9
  92.9 43.0 %fusion = f32[2048,2048]{1,0:T(8,128)} fusion(bf16[2048,4096]{1,0:T(8,128)(2,1)} %all-gather.2.cloned.1.call-done, bf16[4096,2048]{1,0:T(8,128)(2,1)} %param.5), kind=kOutput, calls=%fused_computation.2 | convolution fusion | flops 34359738368 | bytes 50331648 | tf_op jit(solution)/shard_map/dot_general | solution.py:10
  135.9 46.7 %multiply_convert_fusion = bf16[2048,2048]{1,0:T(8,128)(2,1)S(1)} fusion(f32[2048,2048]{1,0:T(8,128)} %fusion, bf16[2048,4096]{1,0:T(8,128)(2,1)} %all-gather.2.cloned.1.call-done, bf16[4096,2048]{1,0:T(8,128)(2,1)} %param.6), kind=kOutput, calls=%fused_computation | convolution fusion | flops 34384904192 | bytes 58720256 | tf_op jit(solution)/shard_map/dot_general | solution.py:11
  182.6 41.0 %convolution_convert_fusion = bf16[2048,4096]{1,0:T(8,128)(2,1)} fusion(bf16[2048,2048]{1,0:T(8,128)(2,1)S(1)} %multiply_convert_fusion, bf16[2048,4096]{1,0:T(8,128)(2,1)} %param.7), kind=kOutput, calls=%fused_computation.1 | convolution fusion | flops 34368126976 | bytes 41943040 | tf_op jit(solution)/shard_map/dot_general | solution.py:13
  223.6 0.1 reduce-scatter.2.cloned.1.call-update
  223.7 88.4 %reduce-scatter.2.cloned.1.call-done = bf16[256,4096]{1,0:T(8,128)(2,1)} async-done(((bf16[2048,4096]{1,0:T(8,128)(2,1)}), bf16[256,4096]{1,0:T(8,128)(2,1)}) %reduce-scatter.2.cloned.1.call-update) | async-done | bytes 2097168 | tf_op jit(solution)/shard_map/reduce_scatter | solution.py:14
Async XLA Ops:
  6.5 86.4 %all-gather.2.cloned.1.call-start = ((), (), s32[]{:S(2)}) async-start(), calls=%async_computation.1 | async-start | bytes 18874368 | tf_op jit(solution)/shard_map/all_gather | solution.py:9
  7.3 304.8 %reduce-scatter.2.cloned.1.call-start = ((), (), s32[]{:S(2)}) async-start(), calls=%async_computation.2 | async-start | bytes 18874368 | tf_op jit(solution)/shard_map/reduce_scatter | solution.py:14
Sparse Core Ops, SparseCore 0:
  8.9 83.9 all-gather.1
  223.8 88.2 reduce-scatter.1
where the time goes:
time: 319 us
  waiting for transfers between devices  175 us (55%)
  matrix products  131 us (41%)
  between operations  13.4 us (4%)
    reduce_scatter x1, waiting for transfers between devices, step(): return lax.psum_scatter(term, 'tp', scatter_dimension=0, tiled=True)  88.4 us
    all_gather x1, waiting for transfers between devices, step(): rows = lax.all_gather(x, 'tp', axis=0, tiled=True)  85.5 us
    dot_general x1, matrix products, step(): up = jnp.dot(rows, w_up, preferred_element_type=jnp.float32)  46.7 us
    dot_general x1, matrix products, step(): gate = jnp.dot(rows, w_gate, preferred_element_type=jnp.float32)  43 us
    dot_general x1, matrix products, step(): jnp.dot(hidden, w_down, preferred_element_type=jnp.float32)  41 us
  transfers between devices with their start and end apart: 2, of which 2 were waited for; matrix products, arithmetic and copies ran while one was open for 0% of the time, Pallas kernels for 0%

commit v1 on v0

v1 whole, which is shorter than its diff:
```python
import functools

import jax
import jax.numpy as jnp
from jax import lax
from jax.experimental import pallas as pl
from jax.experimental.pallas import tpu as pltpu
from jax.sharding import PartitionSpec as P

MESH = pl.DeviceIdType.MESH
BF16, F32 = jnp.bfloat16, jnp.float32
LEFT, RIGHT = 0, 1
TN = 256
TD = 512

STAGES = 6
CHUNKS = STAGES + 2


def kernel(
    n_tp, x_ref, wg_ref, wu_ref, wd_ref,
    own_ref, pt_ref, fl_ref, fr_ref, g_ref, xp_ref, u_ref, ps_ref,
    xv, wguv, wdv, h, ownv, tsend, trecv, psv, uv,
    ag_s, ag_r, dx_s, dx_r, dt_s, dt_r, rs_s, rs_r, lx, wg_sem, wu_sem, wd_sem, own_sem, ps_sem, u_sem,
):
    me = lax.axis_index("tp")
    core = lax.rem(me, 2)
    partner = me + 1 - 2 * core
    to = (lax.rem(me + n_tp - 2, n_tp), lax.rem(me + 2, n_tp))
    rows, d = x_ref.shape
    half, q = rows // 2, rows // 4
    nt, nd = wguv.shape[0], wdv.shape[0]

    def remote(src, dst, send, recv, target):
        return pltpu.make_async_remote_copy(
            src_ref=src, dst_ref=dst, send_sem=send, recv_sem=recv, device_id={"tp": target}, device_id_type=MESH
        )

    def ag(way, s):
        if s in (0, 1):
            src = x_ref.at[pl.ds((s + 2 * way) * q, q)]
        elif s in (2, 3):
            src = g_ref.at[s - 2, pl.ds(way * q, q)]
        else:
            src = x_ref.at[pl.ds((s - 4 + 2 * (1 - way)) * q, q)]
        return remote(src, g_ref.at[s, pl.ds(way * q, q)], ag_s.at[way, s], ag_r.at[way, s], to[way])

    def ag_landed(way, s):
        at = g_ref.at[s, pl.ds(way * q, q)]
        remote(at, at, ag_s.at[way, s], ag_r.at[way, s], to[way]).wait_recv()

    def dx_own(i):
        at = pl.ds(i * half, half)
        return remote(x_ref.at[at], xp_ref.at[at], dx_s.at[STAGES + i], dx_r.at[STAGES + i], partner)

    def dx(s):
        return remote(
            g_ref.at[s, pl.ds(0, half)], g_ref.at[s, pl.ds(half, half)], dx_s.at[s], dx_r.at[s], partner
        )

    def dt(j):
        return remote(tsend, trecv.at[lax.rem(j, 2)], dt_s.at[j], dt_r.at[j], partner)

    def dt_own(i):
        j = i * (CHUNKS - 1)
        return remote(tsend, pt_ref.at[pl.ds(i * half, half)], dt_s.at[j], dt_r.at[j], partner)

    def rs(way, s):
        if s in (0, 1):
            part = 1 - way
            dst = fl_ref.at[pl.ds(s * q, q)] if way == RIGHT else fr_ref.at[pl.ds((2 + s) * q, q)]
        elif s in (2, 3):
            part = way
            dst = u_ref.at[s - 2, pl.ds((1 - way) * q, q)]
        else:
            part = 1 - way
            dst = fl_ref.at[pl.ds((s - 2) * q, q)] if way == RIGHT else fr_ref.at[pl.ds((s - 4) * q, q)]
        return remote(ps_ref.at[s, pl.ds(part * q, q)], dst, rs_s.at[way, s], rs_r.at[way, s], to[way])

    def load_x(j, part):
        at = pl.ds(part * half, half)
        return pltpu.make_async_copy(g_ref.at[j - 1, at], xv.at[lax.rem(j, 2), at], lx.at[part])

    def load_own(i, part):
        src = xp_ref if part else x_ref
        return pltpu.make_async_copy(
            src.at[pl.ds(i * half, half)], xv.at[i, pl.ds(part * half, half)], lx.at[part]
        )

    def load_w(w_ref, part, n, sem):
        return pltpu.make_async_copy(
            w_ref.at[:, pl.ds(n * TN, TN)], wguv.at[n, :, pl.ds(part * TN, TN)], sem.at[n]
        )

    def load_wd(n):
        return pltpu.make_async_copy(wd_ref.at[:, pl.ds(n * TD, TD)], wdv.at[n], wd_sem.at[n])

    def keep_own(i):
        return pltpu.make_async_copy(ownv, own_ref.at[pl.ds(i * half, half)], own_sem.at[0])

    def keep_sum(s):
        return pltpu.make_async_copy(psv, ps_ref.at[s], ps_sem.at[0])

    def load_u(s):
        return pltpu.make_async_copy(u_ref.at[s], uv, u_sem.at[0])

    barrier = pltpu.get_barrier_semaphore()
    for other in (*to, partner):
        pl.semaphore_signal(barrier, inc=1, device_id={"tp": other}, device_id_type=MESH)
    load_own(0, 0).start()
    for n in range(2):
        load_w(wg_ref, 0, n, wg_sem).start()
        load_w(wu_ref, 1, n, wu_sem).start()
    pl.semaphore_wait(barrier, 3)
    dx_own(0).start()
    for s in (0, 1):
        for way in (LEFT, RIGHT):
            ag(way, s).start()
    dx_own(1).start()
    for n in range(2, nt):
        load_w(wg_ref, 0, n, wg_sem).start()
        load_w(wu_ref, 1, n, wu_sem).start()
    for n in range(nd):
        load_wd(n).start()
    dx_own(0).wait_recv()
    load_own(0, 1).start()

    def add_terms(j, upstream):
        def body(c, _):
            at = pl.ds(pl.multiple_of(c * TD, TD), TD)
            total = ownv[:, at] + trecv[lax.rem(j, 2), :, at].astype(F32)
            if upstream:
                total = total + uv[:, at].astype(F32)
            psv[:, at] = total.astype(BF16)
            return 0

        lax.fori_loop(0, d // TD, body, 0)

    def chunk(j, _):
        slot = lax.rem(j, 2)
        before = j - 1
        for part in range(2):
            at = pl.ds(part * half, half)
            pltpu.make_async_copy(g_ref.at[0, at], xv.at[slot, at], lx.at[part]).wait()

        def gate_up(n, _):
            @pl.when(j == 0)
            def _():
                load_w(wg_ref, 0, n, wg_sem).wait()
                load_w(wu_ref, 1, n, wu_sem).wait()

            @pl.when(jnp.logical_and(n == 1, j >= 1))
            def _():
                @pl.when(j == 1)
                def _():
                    dt_own(0).start()
                    keep_own(0).start()

                @pl.when(j > 1)
                def _():
                    dt(before).start()

            @pl.when(jnp.logical_and(n == 4, j >= 6))
            def _():
                for s in (2, 3):
                    @pl.when(j == s + 4)
                    def _():
                        for way in (LEFT, RIGHT):
                            rs(way, s).wait_recv()
                        load_u(s - 2).start()

            @pl.when(jnp.logical_and(n == 5, j >= 1))
            def _():
                @pl.when(j == 1)
                def _():
                    dt_own(0).wait()
                    keep_own(0).wait()

                @pl.when(jnp.logical_and(j > 1, j < 6))
                def _():
                    dt(before).wait()
                    add_terms(before, False)

                @pl.when(j >= 6)
                def _():
                    dt(before).wait()
                    load_u(0).wait()
                    add_terms(before, True)

            @pl.when(jnp.logical_and(n == 6, j >= 2))
            def _():
                keep_sum(j - 2).start()

            @pl.when(jnp.logical_and(n == 7, j >= 2))
            def _():
                keep_sum(j - 2).wait()
                for at, stages in ((2, (0,)), (4, (2,)), (5, (3, 1)), (6, (4,)), (7, (5,))):
                    @pl.when(j == at)
                    def _():
                        for s in stages:
                            for way in (LEFT, RIGHT):
                                rs(way, s).start()

            both = jnp.dot(xv[slot], wguv[n], preferred_element_type=F32)
            gate, up = both[:, :TN], both[:, TN:]
            h[:, pl.ds(pl.multiple_of(n * TN, TN), TN)] = (gate * jax.nn.sigmoid(gate) * up).astype(BF16)
            return 0

        lax.fori_loop(0, nt, gate_up, 0)

        def down(n, _):
            @pl.when(j == 0)
            def _():
                load_wd(n).wait()

            @pl.when(jnp.logical_and(n == 1, j < STAGES))
            def _():
                for way in (LEFT, RIGHT):
                    ag_landed(way, j)
                dx(j).start()
                for s in (0, 1):
                    @pl.when(j == s)
                    def _():
                        for way in (LEFT, RIGHT):
                            ag(way, s + 2).start()

                @pl.when(j == 1)
                def _():
                    for s in (4, 5):
                        for way in (LEFT, RIGHT):
                            ag(way, s).start()

            @pl.when(n == nd - 3)
            def _():
                @pl.when(j < STAGES)
                def _():
                    dx(j).wait_recv()
                    for part in range(2):
                        load_x(j + 1, part).start()

                @pl.when(j == STAGES)
                def _():
                    dx_own(1).wait_recv()
                    for part in range(2):
                        load_own(1, part).start()

            at = pl.ds(pl.multiple_of(n * TD, TD), TD)
            term = jnp.dot(h[...], wdv[n], preferred_element_type=F32)
            ownv[:, at] = term[:half]
            tsend[:, at] = term[half:].astype(BF16)
            return 0

        lax.fori_loop(0, nd, down, 0)
        return 0

    lax.fori_loop(0, CHUNKS, chunk, 0)

    for way in (LEFT, RIGHT):
        for s in (0, 1, 4):
            rs(way, s).wait_recv()
    dt_own(1).start()
    keep_own(1).start()
    for s in range(STAGES):
        for way in (LEFT, RIGHT):
            ag(way, s).wait_send()
        dx(s).wait_send()
    for i in range(2):
        dx_own(i).wait_send()
    dt_own(1).wait()
    keep_own(1).wait()
    for s in range(STAGES):
        for way in (LEFT, RIGHT):
            rs(way, s).wait_send()
    for way in (LEFT, RIGHT):
        rs(way, 5).wait_recv()


def solution(mesh):
    n_tp = mesh.shape["tp"]

    def step(x, w_gate, w_up, w_down):
        rows, d = x.shape
        f = w_gate.shape[1]
        half = rows // 2
        nt, nd = f // TN, d // TD
        shape = jax.ShapeDtypeStruct
        outs = [
            shape((rows, d), F32),
            shape((rows, d), BF16),
            shape((rows, d), BF16),
            shape((rows, d), BF16),
            shape((STAGES, rows, d), BF16),
            shape((rows, d), BF16),
            shape((2, half, d), BF16),
            shape((STAGES, half, d), BF16),
        ]
        dma = pltpu.SemaphoreType.DMA
        own, pt, fl, fr, *_ = pl.pallas_call(
            functools.partial(kernel, n_tp),
            out_shape=outs,
            in_specs=[pl.BlockSpec(memory_space=pl.ANY)] * 4,
            out_specs=[pl.BlockSpec(memory_space=pl.ANY)] * len(outs),
            scratch_shapes=[
                pltpu.VMEM((2, rows, d), BF16),
                pltpu.VMEM((nt, d, 2 * TN), BF16),
                pltpu.VMEM((nd, f, TD), BF16),
                pltpu.VMEM((rows, f), BF16),
                pltpu.VMEM((half, d), F32),
                pltpu.VMEM((half, d), BF16),
                pltpu.VMEM((2, half, d), BF16),
                pltpu.VMEM((half, d), BF16),
                pltpu.VMEM((half, d), BF16),
                dma((2, STAGES)), dma((2, STAGES)),
                dma((CHUNKS,)), dma((CHUNKS,)),
                dma((CHUNKS,)), dma((CHUNKS,)),
                dma((2, STAGES)), dma((2, STAGES)),
                dma((2,)), dma((nt,)), dma((nt,)), dma((nd,)), dma((1,)), dma((1,)), dma((1,)),
            ],
            compiler_params=pltpu.CompilerParams(
                collective_id=0, has_side_effects=True, vmem_limit_bytes=67043328
            ),
            name="mlp_block",
        )(x, w_gate, w_up, w_down)
        total = own + pt.astype(F32) + fl.astype(F32) + fr.astype(F32)
        return total.astype(BF16)

    return jax.shard_map(
        step,
        mesh=mesh,
        in_specs=(P(("dp", "tp"), None), P(None, "tp"), P(None, "tp"), P("tp", None)),
        out_specs=P(("dp", "tp"), None),
        check_vma=False,
    )
```

time: 319 us -> 165 us (0.52)
  waiting for transfers between devices: 175 us -> 0 us
  Pallas kernels: 0 us -> 158 us
  matrix products: 131 us -> 0 us
  between operations: 13.4 us -> 0.01 us
  other arithmetic: 0 us -> 6.65 us
    pallas_call x0 -> x1, Pallas kernels: none -> 158 us  [step(): pl.pallas_call(functools.partial(kernel, n_tp), out_shape=outs, in_specs=...]
    dot_general x3 -> x0, matrix products: 131 us -> none  [the longest x1 46.7 us: step(): up = jnp.dot(rows, w_up, preferred_element_type=jnp.float32)]
    reduce_scatter x1 -> x0, waiting for transfers between devices: 88.4 us -> none  [step(): return lax.psum_scatter(term, 'tp', scatter_dimension=0, tiled=True)]
    all_gather x1 -> x0, waiting for transfers between devices: 85.5 us -> none  [step(): rows = lax.all_gather(x, 'tp', axis=0, tiled=True)]
    convert_element_type x0 -> x1, other arithmetic: none -> 6.65 us  [step(): return total.astype(BF16)]
  transfers between devices with their start and end apart: 2 -> 0, of which waited for: 2 -> 0; matrix products, arithmetic and copies ran while one was open for 0% -> 0% of each run, Pallas kernels for 0% -> 0%
where the time goes in v1:
time: 165 us
  Pallas kernels  158 us (96%)
  other arithmetic  6.65 us (4%)
    pallas_call x1, Pallas kernels, step(): pl.pallas_call(functools.partial(kernel, n_tp), out_shape=outs, in_specs=...  158 us
    convert_element_type x1, other arithmetic, step(): return total.astype(BF16)  6.65 us

profile of v1, /device:TPU:112, one launch (start us, length us, event | category | flops | bytes accessed | tf_op | source)
XLA Modules:
  0.0 164.7 jit_solution(6889190918027732107)
XLA Ops:
  0.0 158.1 %mlp_block.1 = (f32[256,4096]{1,0:T(8,128)}, bf16[256,4096]{1,0:T(8,128)(2,1)}, bf16[256,4096]{1,0:T(8,128)(2,1)}, bf16[256,4096]{1,0:T(8,128)(2,1)}, bf16[6,256...) custom-call(bf16[256,4096]{1,0:T(8,128)(2,1)} %x_ref.1, ...), custom_call_target="tpu_custom_call" | custom-call | tf_op jit(solution)/shard_map/mlp_block/pallas_call | solution.py:298
  158.1 6.6 %add_convert_fusion = bf16[256,4096]{1,0:T(8,128)(2,1)} fusion(bf16[256,4096]{1,0:T(8,128)(2,1)} %get-tuple-element.12, bf16[256,4096]{1,0:T(8,128)(2,1)} %get-tuple-element.11, f32[256,4096]{1,0:T(8,128)} %get-tuple-element.9, bf16[256,4096]{1,0:T(8,128)(2,1)} %get-tuple-element.10), kind=kLoop, calls=%fused_computation | loop fusion | flops 7340032 | bytes 12582912 | tf_op jit(solution)/shard_map/convert_element_type | solution.py:325

commit v2 on v1

--- a/solution.py
+++ b/solution.py
@@ -12,6 +12,7 @@
 LEFT, RIGHT = 0, 1
 TN = 256
 TD = 512
+UNROLL = 2
 
 STAGES = 6
 CHUNKS = STAGES + 2
@@ -95,6 +96,15 @@
     def load_wd(n):
         return pltpu.make_async_copy(wd_ref.at[:, pl.ds(n * TD, TD)], wdv.at[n], wd_sem.at[n])
 
+    def load_gate_up(m):
+        for i in range(UNROLL):
+            load_w(wg_ref, 0, m * UNROLL + i, wg_sem).start()
+            load_w(wu_ref, 1, m * UNROLL + i, wu_sem).start()
+
+    def load_down(m):
+        for i in range(UNROLL):
+            load_wd(m * UNROLL + i).start()
+
     def keep_own(i):
         return pltpu.make_async_copy(ownv, own_ref.at[pl.ds(i * half, half)], own_sem.at[0])
 
@@ -108,22 +118,16 @@
     for other in (*to, partner):
         pl.semaphore_signal(barrier, inc=1, device_id={"tp": other}, device_id_type=MESH)
     load_own(0, 0).start()
-    for n in range(2):
-        load_w(wg_ref, 0, n, wg_sem).start()
-        load_w(wu_ref, 1, n, wu_sem).start()
+    load_gate_up(0)
     pl.semaphore_wait(barrier, 3)
     dx_own(0).start()
     for s in (0, 1):
         for way in (LEFT, RIGHT):
             ag(way, s).start()
     dx_own(1).start()
-    for n in range(2, nt):
-        load_w(wg_ref, 0, n, wg_sem).start()
-        load_w(wu_ref, 1, n, wu_sem).start()
-    for n in range(nd):
-        load_wd(n).start()
     dx_own(0).wait_recv()
     load_own(0, 1).start()
+    load_gate_up(1)
 
     def add_terms(j, upstream):
         def body(c, _):
@@ -143,13 +147,22 @@
             at = pl.ds(part * half, half)
             pltpu.make_async_copy(g_ref.at[0, at], xv.at[slot, at], lx.at[part]).wait()
 
-        def gate_up(n, _):
+        def gate_up(m, _):
             @pl.when(j == 0)
             def _():
-                load_w(wg_ref, 0, n, wg_sem).wait()
-                load_w(wu_ref, 1, n, wu_sem).wait()
-
-            @pl.when(jnp.logical_and(n == 1, j >= 1))
+                for i in range(UNROLL):
+                    load_w(wg_ref, 0, m * UNROLL + i, wg_sem).wait()
+                    load_w(wu_ref, 1, m * UNROLL + i, wu_sem).wait()
+
+                @pl.when(m + 2 < nt // UNROLL)
+                def _():
+                    load_gate_up(m + 2)
+
+                @pl.when(m + 2 >= nt // UNROLL)
+                def _():
+                    load_down(m + 2 - nt // UNROLL)
+
+            @pl.when(jnp.logical_and(m == 1, j >= 1))
             def _():
                 @pl.when(j == 1)
                 def _():
@@ -160,7 +173,7 @@
                 def _():
                     dt(before).start()
 
-            @pl.when(jnp.logical_and(n == 4, j >= 6))
+            @pl.when(jnp.logical_and(m == 2, j >= 6))
             def _():
                 for s in (2, 3):
                     @pl.when(j == s + 4)
@@ -169,7 +182,7 @@
                             rs(way, s).wait_recv()
                         load_u(s - 2).start()
 
-            @pl.when(jnp.logical_and(n == 5, j >= 1))
+            @pl.when(jnp.logical_and(m == 3, j >= 1))
             def _():
                 @pl.when(j == 1)
                 def _():
@@ -187,11 +200,55 @@
                     load_u(0).wait()
                     add_terms(before, True)
 
-            @pl.when(jnp.logical_and(n == 6, j >= 2))
-            def _():
-                keep_sum(j - 2).start()
-
-            @pl.when(jnp.logical_and(n == 7, j >= 2))
+            for i in range(UNROLL):
+                n = m * UNROLL + i
+                both = jnp.dot(xv[slot], wguv[n], preferred_element_type=F32)
+                gate, up = both[:, :TN], both[:, TN:]
+                h[:, pl.ds(pl.multiple_of(n * TN, TN), TN)] = (gate * jax.nn.sigmoid(gate) * up).astype(BF16)
+            return 0
+
+        lax.fori_loop(0, nt // UNROLL, gate_up, 0)
+
+        def down(m, _):
+            @pl.when(j == 0)
+            def _():
+                for i in range(UNROLL):
+                    load_wd(m * UNROLL + i).wait()
+
+                @pl.when(m + 2 < nd // UNROLL)
+                def _():
+                    load_down(m + 2)
+
+            @pl.when(m == 0)
+            def _():
+                @pl.when(j < STAGES)
+                def _():
+                    for way in (LEFT, RIGHT):
+                        ag_landed(way, j)
+                    dx(j).start()
+                    for s in (0, 1):
+                        @pl.when(j == s)
+                        def _():
+                            for way in (LEFT, RIGHT):
+                                ag(way, s + 2).start()
+
+                    @pl.when(j == 1)
+                    def _():
+                        for s in (4, 5):
+                            for way in (LEFT, RIGHT):
+                                ag(way, s).start()
+
+                    load_x(j + 1, 0).start()
+
+                @pl.when(j == STAGES)
+                def _():
+                    load_own(1, 0).start()
+
+                @pl.when(j >= 2)
+                def _():
+                    keep_sum(j - 2).start()
+
+            @pl.when(jnp.logical_and(m == 1, j >= 2))
             def _():
                 keep_sum(j - 2).wait()
                 for at, stages in ((2, (0,)), (4, (2,)), (5, (3, 1)), (6, (4,)), (7, (5,))):
@@ -201,56 +258,27 @@
                             for way in (LEFT, RIGHT):
                                 rs(way, s).start()
 
-            both = jnp.dot(xv[slot], wguv[n], preferred_element_type=F32)
-            gate, up = both[:, :TN], both[:, TN:]
-            h[:, pl.ds(pl.multiple_of(n * TN, TN), TN)] = (gate * jax.nn.sigmoid(gate) * up).astype(BF16)
+            @pl.when(m == 2)
+            def _():
+                @pl.when(j < STAGES)
+                def _():
+                    dx(j).wait_recv()
+                    load_x(j + 1, 1).start()
+
+                @pl.when(j == STAGES)
+                def _():
+                    dx_own(1).wait_recv()
+                    load_own(1, 1).start()
+
+            for i in range(UNROLL):
+                n = m * UNROLL + i
+                at = pl.ds(pl.multiple_of(n * TD, TD), TD)
+                term = jnp.dot(h[...], wdv[n], preferred_element_type=F32)
+                ownv[:, at] = term[:half]
+                tsend[:, at] = term[half:].astype(BF16)
             return 0
 
-        lax.fori_loop(0, nt, gate_up, 0)
-
-        def down(n, _):
-            @pl.when(j == 0)
-            def _():
-                load_wd(n).wait()
-
-            @pl.when(jnp.logical_and(n == 1, j < STAGES))
-            def _():
-                for way in (LEFT, RIGHT):
-                    ag_landed(way, j)
-                dx(j).start()
-                for s in (0, 1):
-                    @pl.when(j == s)
-                    def _():
-                        for way in (LEFT, RIGHT):
-                            ag(way, s + 2).start()
-
-                @pl.when(j == 1)
-                def _():
-                    for s in (4, 5):
-                        for way in (LEFT, RIGHT):
-                            ag(way, s).start()
-
-            @pl.when(n == nd - 3)
-            def _():
-                @pl.when(j < STAGES)
-                def _():
-                    dx(j).wait_recv()
-                    for part in range(2):
-                        load_x(j + 1, part).start()
-
-                @pl.when(j == STAGES)
-                def _():
-                    dx_own(1).wait_recv()
-                    for part in range(2):
-                        load_own(1, part).start()
-
-            at = pl.ds(pl.multiple_of(n * TD, TD), TD)
-            term = jnp.dot(h[...], wdv[n], preferred_element_type=F32)
-            ownv[:, at] = term[:half]
-            tsend[:, at] = term[half:].astype(BF16)
-            return 0
-
-        lax.fori_loop(0, nd, down, 0)
+        lax.fori_loop(0, nd // UNROLL, down, 0)
         return 0
 
     lax.fori_loop(0, CHUNKS, chunk, 0)

time: 165 us -> 150 us (0.909)
  Pallas kernels: 158 us -> 143 us
    pallas_call x1, Pallas kernels: 158 us -> 143 us  [step(): pl.pallas_call(functools.partial(kernel, n_tp), out_shape=outs, in_specs=...]
where the time goes in v2:
time: 150 us
  Pallas kernels  143 us (95%)
  other arithmetic  6.65 us (4%)
    pallas_call x1, Pallas kernels, step(): pl.pallas_call(functools.partial(kernel, n_tp), out_shape=outs, in_specs=...  143 us
    convert_element_type x1, other arithmetic, step(): return total.astype(BF16)  6.65 us

profile of v2, /device:TPU:112, one launch (start us, length us, event | category | flops | bytes accessed | tf_op | source)
XLA Modules:
  0.0 149.6 jit_solution(10408258745747742322)
XLA Ops:
  0.0 143.0 %mlp_block.1 = (f32[256,4096]{1,0:T(8,128)}, bf16[256,4096]{1,0:T(8,128)(2,1)}, bf16[256,4096]{1,0:T(8,128)(2,1)}, bf16[256,4096]{1,0:T(8,128)(2,1)}, bf16[6,256...) custom-call(bf16[256,4096]{1,0:T(8,128)(2,1)} %x_ref.1, ...), custom_call_target="tpu_custom_call" | custom-call | tf_op jit(solution)/shard_map/mlp_block/pallas_call | solution.py:326
  143.0 6.6 %add_convert_fusion = bf16[256,4096]{1,0:T(8,128)(2,1)} fusion(bf16[256,4096]{1,0:T(8,128)(2,1)} %get-tuple-element.12, bf16[256,4096]{1,0:T(8,128)(2,1)} %get-tuple-element.11, f32[256,4096]{1,0:T(8,128)} %get-tuple-element.9, bf16[256,4096]{1,0:T(8,128)(2,1)} %get-tuple-element.10), kind=kLoop, calls=%fused_computation | loop fusion | flops 7340032 | bytes 12582912 | tf_op jit(solution)/shard_map/convert_element_type | solution.py:353

commit v3 on v2

--- a/solution.py
+++ b/solution.py
@@ -20,9 +20,9 @@
 
 def kernel(
     n_tp, x_ref, wg_ref, wu_ref, wd_ref,
-    own_ref, pt_ref, fl_ref, fr_ref, g_ref, xp_ref, u_ref, ps_ref,
-    xv, wguv, wdv, h, ownv, tsend, trecv, psv, uv,
-    ag_s, ag_r, dx_s, dx_r, dt_s, dt_r, rs_s, rs_r, lx, wg_sem, wu_sem, wd_sem, own_sem, ps_sem, u_sem,
+    y_ref, fl_ref, fr_ref, g_ref, xp_ref, u_ref, ps_ref,
+    xv, wguv, wdv, h, ownv, tsend, trecv, uv, last,
+    ag_s, ag_r, dx_s, dx_r, dt_s, dt_r, rs_s, rs_r, lx, wg_sem, wu_sem, wd_sem, y_sem, ps_sem, u_sem,
 ):
     me = lax.axis_index("tp")
     core = lax.rem(me, 2)
@@ -62,10 +62,6 @@
     def dt(j):
         return remote(tsend, trecv.at[lax.rem(j, 2)], dt_s.at[j], dt_r.at[j], partner)
 
-    def dt_own(i):
-        j = i * (CHUNKS - 1)
-        return remote(tsend, pt_ref.at[pl.ds(i * half, half)], dt_s.at[j], dt_r.at[j], partner)
-
     def rs(way, s):
         if s in (0, 1):
             part = 1 - way
@@ -73,9 +69,12 @@
         elif s in (2, 3):
             part = way
             dst = u_ref.at[s - 2, pl.ds((1 - way) * q, q)]
+        elif s == 4:
+            part = 1 - way
+            dst = fl_ref.at[pl.ds(2 * q, q)] if way == RIGHT else fr_ref.at[pl.ds(0, q)]
         else:
             part = 1 - way
-            dst = fl_ref.at[pl.ds((s - 2) * q, q)] if way == RIGHT else fr_ref.at[pl.ds((s - 4) * q, q)]
+            dst = last.at[way]
         return remote(ps_ref.at[s, pl.ds(part * q, q)], dst, rs_s.at[way, s], rs_r.at[way, s], to[way])
 
     def load_x(j, part):
@@ -105,11 +104,8 @@
         for i in range(UNROLL):
             load_wd(m * UNROLL + i).start()
 
-    def keep_own(i):
-        return pltpu.make_async_copy(ownv, own_ref.at[pl.ds(i * half, half)], own_sem.at[0])
-
     def keep_sum(s):
-        return pltpu.make_async_copy(psv, ps_ref.at[s], ps_sem.at[0])
+        return pltpu.make_async_copy(trecv.at[lax.rem(s + 1, 2)], ps_ref.at[s], ps_sem.at[0])
 
     def load_u(s):
         return pltpu.make_async_copy(u_ref.at[s], uv, u_sem.at[0])
@@ -129,16 +125,27 @@
     load_own(0, 1).start()
     load_gate_up(1)
 
+    def columns(body):
+        def step(c, _):
+            body(pl.ds(pl.multiple_of(c * TD, TD), TD))
+            return 0
+
+        lax.fori_loop(0, d // TD, step, 0)
+
     def add_terms(j, upstream):
-        def body(c, _):
-            at = pl.ds(pl.multiple_of(c * TD, TD), TD)
-            total = ownv[:, at] + trecv[lax.rem(j, 2), :, at].astype(F32)
+        def body(at):
+            total = ownv[1, :, at] + trecv[lax.rem(j, 2), :, at].astype(F32)
             if upstream:
                 total = total + uv[:, at].astype(F32)
-            psv[:, at] = total.astype(BF16)
-            return 0
-
-        lax.fori_loop(0, d // TD, body, 0)
+            trecv[lax.rem(j, 2), :, at] = total.astype(BF16)
+
+        columns(body)
+
+    def add_own(i, part):
+        def body(at):
+            ownv[i, :, at] = ownv[i, :, at] + part(at).astype(F32)
+
+        columns(body)
 
     def chunk(j, _):
         slot = lax.rem(j, 2)
@@ -164,14 +171,7 @@
 
             @pl.when(jnp.logical_and(m == 1, j >= 1))
             def _():
-                @pl.when(j == 1)
-                def _():
-                    dt_own(0).start()
-                    keep_own(0).start()
-
-                @pl.when(j > 1)
-                def _():
-                    dt(before).start()
+                dt(before).start()
 
             @pl.when(jnp.logical_and(m == 2, j >= 6))
             def _():
@@ -184,19 +184,18 @@
 
             @pl.when(jnp.logical_and(m == 3, j >= 1))
             def _():
+                dt(before).wait()
+
                 @pl.when(j == 1)
                 def _():
-                    dt_own(0).wait()
-                    keep_own(0).wait()
+                    add_own(0, lambda at: trecv[0, :, at])
 
                 @pl.when(jnp.logical_and(j > 1, j < 6))
                 def _():
-                    dt(before).wait()
                     add_terms(before, False)
 
                 @pl.when(j >= 6)
                 def _():
-                    dt(before).wait()
                     load_u(0).wait()
                     add_terms(before, True)
 
@@ -274,7 +273,7 @@
                 n = m * UNROLL + i
                 at = pl.ds(pl.multiple_of(n * TD, TD), TD)
                 term = jnp.dot(h[...], wdv[n], preferred_element_type=F32)
-                ownv[:, at] = term[:half]
+                ownv[lax.min(j, 1), :, at] = term[:half]
                 tsend[:, at] = term[half:].astype(BF16)
             return 0
 
@@ -283,24 +282,70 @@
 
     lax.fori_loop(0, CHUNKS, chunk, 0)
 
+    def fetch(src, dst, i):
+        return pltpu.make_async_copy(src, dst, lx.at[i])
+
+    def put(i, src):
+        return pltpu.make_async_copy(src, y_ref.at[pl.ds(i * q, q)], y_sem.at[i])
+
+    def finish(dst, acc, part, rows_at):
+        def body(at):
+            dst[:, at] = (ownv[acc, rows_at, at] + part(at).astype(F32)).astype(BF16)
+
+        columns(body)
+
+    top, bottom = pl.ds(0, q), pl.ds(q, q)
+    first, second = pl.ds(0, half), pl.ds(half, half)
+
+    for s in (0, 1):
+        for way in (LEFT, RIGHT):
+            rs(way, s).wait_recv()
+    loads = fetch(fl_ref.at[first], xv.at[0, first], 0), fetch(fr_ref.at[second], xv.at[0, second], 1)
+    for load in loads:
+        load.start()
+    for load in loads:
+        load.wait()
+    dt(CHUNKS - 1).start()
+    add_own(0, lambda at: xv[0, first, at])
+    add_own(1, lambda at: xv[0, second, at])
+    dt(CHUNKS - 1).wait()
+    add_own(1, lambda at: trecv[(CHUNKS - 1) % 2, :, at])
+
     for way in (LEFT, RIGHT):
-        for s in (0, 1, 4):
-            rs(way, s).wait_recv()
-    dt_own(1).start()
-    keep_own(1).start()
+        rs(way, 4).wait_recv()
+    loads = fetch(fr_ref.at[top], xv.at[1, top], 0), fetch(fl_ref.at[pl.ds(half, q)], xv.at[1, bottom], 1)
+    for load in loads:
+        load.start()
+    for load in loads:
+        load.wait()
+    finish(tsend.at[top], 0, lambda at: xv[1, top, at], top)
+    put(0, tsend.at[top]).start()
+    finish(tsend.at[bottom], 1, lambda at: xv[1, bottom, at], top)
+    put(2, tsend.at[bottom]).start()
+
     for s in range(STAGES):
         for way in (LEFT, RIGHT):
             ag(way, s).wait_send()
         dx(s).wait_send()
     for i in range(2):
         dx_own(i).wait_send()
-    dt_own(1).wait()
-    keep_own(1).wait()
-    for s in range(STAGES):
+    for s in range(STAGES - 1):
         for way in (LEFT, RIGHT):
             rs(way, s).wait_send()
+    put(0, tsend.at[top]).wait()
+    put(2, tsend.at[bottom]).wait()
+
+    done = trecv.at[0]
+    rs(LEFT, 5).wait_recv()
+    finish(done.at[top], 0, lambda at: last[LEFT, :, at], bottom)
+    put(1, done.at[top]).start()
+    rs(RIGHT, 5).wait_recv()
+    finish(done.at[bottom], 1, lambda at: last[RIGHT, :, at], bottom)
+    put(3, done.at[bottom]).start()
     for way in (LEFT, RIGHT):
-        rs(way, 5).wait_recv()
+        rs(way, 5).wait_send()
+    put(1, done.at[top]).wait()
+    put(3, done.at[bottom]).wait()
 
 
 def solution(mesh):
@@ -313,7 +358,6 @@
         nt, nd = f // TN, d // TD
         shape = jax.ShapeDtypeStruct
         outs = [
-            shape((rows, d), F32),
             shape((rows, d), BF16),
             shape((rows, d), BF16),
             shape((rows, d), BF16),
@@ -323,7 +367,7 @@
             shape((STAGES, half, d), BF16),
         ]
         dma = pltpu.SemaphoreType.DMA
-        own, pt, fl, fr, *_ = pl.pallas_call(
+        y, *_ = pl.pallas_call(
             functools.partial(kernel, n_tp),
             out_shape=outs,
             in_specs=[pl.BlockSpec(memory_space=pl.ANY)] * 4,
@@ -333,24 +377,23 @@
                 pltpu.VMEM((nt, d, 2 * TN), BF16),
                 pltpu.VMEM((nd, f, TD), BF16),
                 pltpu.VMEM((rows, f), BF16),
-                pltpu.VMEM((half, d), F32),
+                pltpu.VMEM((2, half, d), F32),
                 pltpu.VMEM((half, d), BF16),
                 pltpu.VMEM((2, half, d), BF16),
                 pltpu.VMEM((half, d), BF16),
-                pltpu.VMEM((half, d), BF16),
+                pltpu.VMEM((2, rows // 4, d), BF16),
                 dma((2, STAGES)), dma((2, STAGES)),
                 dma((CHUNKS,)), dma((CHUNKS,)),
                 dma((CHUNKS,)), dma((CHUNKS,)),
                 dma((2, STAGES)), dma((2, STAGES)),
-                dma((2,)), dma((nt,)), dma((nt,)), dma((nd,)), dma((1,)), dma((1,)), dma((1,)),
+                dma((2,)), dma((nt,)), dma((nt,)), dma((nd,)), dma((4,)), dma((1,)), dma((1,)),
             ],
             compiler_params=pltpu.CompilerParams(
                 collective_id=0, has_side_effects=True, vmem_limit_bytes=67043328
             ),
             name="mlp_block",
         )(x, w_gate, w_up, w_down)
-        total = own + pt.astype(F32) + fl.astype(F32) + fr.astype(F32)
-        return total.astype(BF16)
+        return y
 
     return jax.shard_map(
         step,

time: 150 us -> 147 us (0.980)
  other arithmetic: 6.65 us -> 0 us
  local copies, waits for them, and re-layouts: 0 us -> 3.13 us
    convert_element_type x1 -> x0, other arithmetic: 6.65 us -> none  [step(): return total.astype(BF16)]
    unnamed x0 -> x1, local copies, waits for them, and re-layouts: none -> 3.13 us
where the time goes in v3:
time: 147 us
  Pallas kernels  144 us (98%)
  local copies, waits for them, and re-layouts  3.13 us (2%)
    pallas_call x1, Pallas kernels, step(): pl.pallas_call(functools.partial(kernel, n_tp), out_shape=outs, in_specs=...  144 us
    unnamed x1, local copies, waits for them, and re-layouts  3.13 us

profile of v3, /device:TPU:112, one launch (start us, length us, event | category | flops | bytes accessed | tf_op | source)
XLA Modules:
  0.0 147.3 jit_solution(7754158849496202)
XLA Ops:
  0.0 144.1 %mlp_block.1 = (bf16[256,4096]{1,0:T(8,128)(2,1)}, bf16[256,4096]{1,0:T(8,128)(2,1)}, bf16[256,4096]{1,0:T(8,128)(2,1)}, bf16[6,256,4096]{2,1,0:T(8,128)(2,1)}, ...) custom-call(bf16[256,4096]{1,0:T(8,128)(2,1)} %x_ref.1, ...), custom_call_target="tpu_custom_call" | custom-call | tf_op jit(solution)/shard_map/mlp_block/pallas_call | solution.py:370
  144.1 3.1 %copy.6 = bf16[256,4096]{1,0:T(8,128)(2,1)} copy(bf16[256,4096]{1,0:T(8,128)(2,1)} %get-tuple-element.6) | data formatting | bytes 4194304

commit v4 on v3

--- a/solution.py
+++ b/solution.py
@@ -21,8 +21,8 @@
 def kernel(
     n_tp, x_ref, wg_ref, wu_ref, wd_ref,
     y_ref, fl_ref, fr_ref, g_ref, xp_ref, u_ref, ps_ref,
-    xv, wguv, wdv, h, ownv, tsend, trecv, uv, last,
-    ag_s, ag_r, dx_s, dx_r, dt_s, dt_r, rs_s, rs_r, lx, wg_sem, wu_sem, wd_sem, y_sem, ps_sem, u_sem,
+    xv, wguv, wdv, h, ownv, tsend, uv, last,
+    ag_s, ag_r, dx_s, dx_r, dt_s, dt_r, rs_s, rs_r, lx, wg_sem, wu_sem, wd_sem, ps_sem, u_sem,
 ):
     me = lax.axis_index("tp")
     core = lax.rem(me, 2)
@@ -31,6 +31,7 @@
     rows, d = x_ref.shape
     half, q = rows // 2, rows // 4
     nt, nd = wguv.shape[0], wdv.shape[0]
+    trecv = y_ref
 
     def remote(src, dst, send, recv, target):
         return pltpu.make_async_remote_copy(
@@ -285,9 +286,6 @@
     def fetch(src, dst, i):
         return pltpu.make_async_copy(src, dst, lx.at[i])
 
-    def put(i, src):
-        return pltpu.make_async_copy(src, y_ref.at[pl.ds(i * q, q)], y_sem.at[i])
-
     def finish(dst, acc, part, rows_at):
         def body(at):
             dst[:, at] = (ownv[acc, rows_at, at] + part(at).astype(F32)).astype(BF16)
@@ -318,10 +316,8 @@
         load.start()
     for load in loads:
         load.wait()
-    finish(tsend.at[top], 0, lambda at: xv[1, top, at], top)
-    put(0, tsend.at[top]).start()
-    finish(tsend.at[bottom], 1, lambda at: xv[1, bottom, at], top)
-    put(2, tsend.at[bottom]).start()
+    finish(y_ref.at[0, top], 0, lambda at: xv[1, top, at], top)
+    finish(y_ref.at[1, top], 1, lambda at: xv[1, bottom, at], top)
 
     for s in range(STAGES):
         for way in (LEFT, RIGHT):
@@ -332,20 +328,11 @@
     for s in range(STAGES - 1):
         for way in (LEFT, RIGHT):
             rs(way, s).wait_send()
-    put(0, tsend.at[top]).wait()
-    put(2, tsend.at[bottom]).wait()
-
-    done = trecv.at[0]
-    rs(LEFT, 5).wait_recv()
-    finish(done.at[top], 0, lambda at: last[LEFT, :, at], bottom)
-    put(1, done.at[top]).start()
-    rs(RIGHT, 5).wait_recv()
-    finish(done.at[bottom], 1, lambda at: last[RIGHT, :, at], bottom)
-    put(3, done.at[bottom]).start()
+    for way in (LEFT, RIGHT):
+        rs(way, 5).wait_recv()
+        finish(y_ref.at[way, bottom], way, lambda at, way=way: last[way, :, at], bottom)
     for way in (LEFT, RIGHT):
         rs(way, 5).wait_send()
-    put(1, done.at[top]).wait()
-    put(3, done.at[bottom]).wait()
 
 
 def solution(mesh):
@@ -358,7 +345,7 @@
         nt, nd = f // TN, d // TD
         shape = jax.ShapeDtypeStruct
         outs = [
-            shape((rows, d), BF16),
+            pltpu.VMEM((2, half, d), BF16),
             shape((rows, d), BF16),
             shape((rows, d), BF16),
             shape((STAGES, rows, d), BF16),
@@ -371,7 +358,7 @@
             functools.partial(kernel, n_tp),
             out_shape=outs,
             in_specs=[pl.BlockSpec(memory_space=pl.ANY)] * 4,
-            out_specs=[pl.BlockSpec(memory_space=pl.ANY)] * len(outs),
+            out_specs=[pl.BlockSpec(memory_space=pltpu.VMEM)] + [pl.BlockSpec(memory_space=pl.ANY)] * (len(outs) - 1),
             scratch_shapes=[
                 pltpu.VMEM((2, rows, d), BF16),
                 pltpu.VMEM((nt, d, 2 * TN), BF16),
@@ -379,21 +366,20 @@
                 pltpu.VMEM((rows, f), BF16),
                 pltpu.VMEM((2, half, d), F32),
                 pltpu.VMEM((half, d), BF16),
-                pltpu.VMEM((2, half, d), BF16),
                 pltpu.VMEM((half, d), BF16),
                 pltpu.VMEM((2, rows // 4, d), BF16),
                 dma((2, STAGES)), dma((2, STAGES)),
                 dma((CHUNKS,)), dma((CHUNKS,)),
                 dma((CHUNKS,)), dma((CHUNKS,)),
                 dma((2, STAGES)), dma((2, STAGES)),
-                dma((2,)), dma((nt,)), dma((nt,)), dma((nd,)), dma((4,)), dma((1,)), dma((1,)),
+                dma((2,)), dma((nt,)), dma((nt,)), dma((nd,)), dma((1,)), dma((1,)),
             ],
             compiler_params=pltpu.CompilerParams(
-                collective_id=0, has_side_effects=True, vmem_limit_bytes=67043328
+                collective_id=0, has_side_effects=True, vmem_limit_bytes=64900000
             ),
             name="mlp_block",
         )(x, w_gate, w_up, w_down)
-        return y
+        return y.reshape(rows, d)
 
     return jax.shard_map(
         step,

time: 147 us -> 145 us (0.986)
  local copies, waits for them, and re-layouts: 3.13 us -> 1.32 us
    unnamed x1, local copies, waits for them, and re-layouts: 3.13 us -> 1.32 us
where the time goes in v4:
time: 145 us
  Pallas kernels  143 us (99%)
    pallas_call x1, Pallas kernels, step(): pl.pallas_call(functools.partial(kernel, n_tp), out_shape=outs, in_specs=...  143 us

profile of v4, /device:TPU:112, one launch (start us, length us, event | category | flops | bytes accessed | tf_op | source)
XLA Modules:
  0.0 144.7 jit_solution(8098215795046776906)
XLA Ops:
  0.0 143.4 %mlp_block.1 = (bf16[2,128,4096]{2,1,0:T(8,128)(2,1)S(1)}, bf16[256,4096]{1,0:T(8,128)(2,1)}, bf16[256,4096]{1,0:T(8,128)(2,1)}, bf16[6,256,4096]{2,1,0:T(8,128)...) custom-call(bf16[256,4096]{1,0:T(8,128)(2,1)} %x_ref.1, ...), custom_call_target="tpu_custom_call" | custom-call | tf_op jit(solution)/shard_map/mlp_block/pallas_call | solution.py:357
  143.4 1.3 copy.6

commit v5 on v4

--- a/solution.py
+++ b/solution.py
@@ -117,11 +117,10 @@
     load_own(0, 0).start()
     load_gate_up(0)
     pl.semaphore_wait(barrier, 3)
-    dx_own(0).start()
     for s in (0, 1):
         for way in (LEFT, RIGHT):
             ag(way, s).start()
-    dx_own(1).start()
+        dx_own(s).start()
     dx_own(0).wait_recv()
     load_own(0, 1).start()
     load_gate_up(1)
@@ -251,7 +250,7 @@
             @pl.when(jnp.logical_and(m == 1, j >= 2))
             def _():
                 keep_sum(j - 2).wait()
-                for at, stages in ((2, (0,)), (4, (2,)), (5, (3, 1)), (6, (4,)), (7, (5,))):
+                for at, stages in ((2, (0,)), (4, (2, 1)), (5, (3,)), (6, (4,)), (7, (5,))):
                     @pl.when(j == at)
                     def _():
                         for s in stages:

time: 145 us -> 143 us (0.986)
  Pallas kernels: 143 us -> 141 us
    pallas_call x1, Pallas kernels: 143 us -> 141 us  [step(): pl.pallas_call(functools.partial(kernel, n_tp), out_shape=outs, in_specs=...]
where the time goes in v5:
time: 143 us; the launch traced here: 142 us
  Pallas kernels  141 us (99%)
    pallas_call x1, Pallas kernels, step(): pl.pallas_call(functools.partial(kernel, n_tp), out_shape=outs, in_specs=...  141 us

profile of v5, /device:TPU:112, one launch (start us, length us, event | category | flops | bytes accessed | tf_op | source)
XLA Modules:
  0.0 142.5 jit_solution(11791222017341551362)
XLA Ops:
  0.0 141.2 %mlp_block.1 = (bf16[2,128,4096]{2,1,0:T(8,128)(2,1)S(1)}, bf16[256,4096]{1,0:T(8,128)(2,1)}, bf16[256,4096]{1,0:T(8,128)(2,1)}, bf16[6,256,4096]{2,1,0:T(8,128)...) custom-call(bf16[256,4096]{1,0:T(8,128)(2,1)} %x_ref.1, ...), custom_call_target="tpu_custom_call" | custom-call | tf_op jit(solution)/shard_map/mlp_block/pallas_call | solution.py:356
  141.2 1.3 copy.6

commit v6 on v5

--- a/solution.py
+++ b/solution.py
@@ -11,7 +11,7 @@
 BF16, F32 = jnp.bfloat16, jnp.float32
 LEFT, RIGHT = 0, 1
 TN = 256
-TD = 512
+TD = 1024
 UNROLL = 2
 
 STAGES = 6
@@ -147,6 +147,24 @@
 
         columns(body)
 
+    def pass_on(j):
+        for way in (LEFT, RIGHT):
+            ag_landed(way, j)
+        dx(j).start()
+        for s in (0, 1):
+            @pl.when(j == s)
+            def _():
+                for way in (LEFT, RIGHT):
+                    ag(way, s + 2).start()
+
+        @pl.when(j == 1)
+        def _():
+            for s in (4, 5):
+                for way in (LEFT, RIGHT):
+                    ag(way, s).start()
+
+        load_x(j + 1, 0).start()
+
     def chunk(j, _):
         slot = lax.rem(j, 2)
         before = j - 1
@@ -199,6 +217,10 @@
                     load_u(0).wait()
                     add_terms(before, True)
 
+            @pl.when(jnp.logical_and(m == 3, jnp.logical_and(j >= 1, j < STAGES)))
+            def _():
+                pass_on(j)
+
             for i in range(UNROLL):
                 n = m * UNROLL + i
                 both = jnp.dot(xv[slot], wguv[n], preferred_element_type=F32)
@@ -220,24 +242,9 @@
 
             @pl.when(m == 0)
             def _():
-                @pl.when(j < STAGES)
-                def _():
-                    for way in (LEFT, RIGHT):
-                        ag_landed(way, j)
-                    dx(j).start()
-                    for s in (0, 1):
-                        @pl.when(j == s)
-                        def _():
-                            for way in (LEFT, RIGHT):
-                                ag(way, s + 2).start()
-
-                    @pl.when(j == 1)
-                    def _():
-                        for s in (4, 5):
-                            for way in (LEFT, RIGHT):
-                                ag(way, s).start()
-
-                    load_x(j + 1, 0).start()
+                @pl.when(j == 0)
+                def _():
+                    pass_on(jnp.int32(0))
 
                 @pl.when(j == STAGES)
                 def _():
@@ -257,7 +264,7 @@
                             for way in (LEFT, RIGHT):
                                 rs(way, s).start()
 
-            @pl.when(m == 2)
+            @pl.when(m == 1)
             def _():
                 @pl.when(j < STAGES)
                 def _():

time: 143 us -> 143 us (level)
  no operation moved by 1% of the time
where the time goes in v6:
time: 143 us; the launch traced here: 142 us
  Pallas kernels  141 us (99%)
    pallas_call x1, Pallas kernels, step(): pl.pallas_call(functools.partial(kernel, n_tp), out_shape=outs, in_specs=...  141 us

profile of v6, /device:TPU:112, one launch (start us, length us, event | category | flops | bytes accessed | tf_op | source)
XLA Modules:
  0.0 142.4 jit_solution(16284465921915911834)
XLA Ops:
  0.0 141.1 %mlp_block.1 = (bf16[2,128,4096]{2,1,0:T(8,128)(2,1)S(1)}, bf16[256,4096]{1,0:T(8,128)(2,1)}, bf16[256,4096]{1,0:T(8,128)(2,1)}, bf16[6,256,4096]{2,1,0:T(8,128)...) custom-call(bf16[256,4096]{1,0:T(8,128)(2,1)} %x_ref.1, ...), custom_call_target="tpu_custom_call" | custom-call | tf_op jit(solution)/shard_map/mlp_block/pallas_call | solution.py:363
  141.1 1.3 copy.6
